TPU v7x, 256 devices: a whole 4x4x8 slice. The times are simulated.
256 devices in a mesh: row: 8 (over y, z_lo), col: 8 (over z_hi, core), layer: 4 (over x).
Axes of the slice: x: 4, y: 4, z: 8 (z_hi: 4, z_lo: 2; z = z_hi * 2 + z_lo), core: 2. Of those that a mesh axis runs over, the one named last changes fastest.
Arguments:
- density_tiles: bfloat16 [192, 8, 2, 128, 128], P(('row', 'col')), may hold values from -1.5 to 1.5
- tile_columns: int32 [192, 8, 2], P(('row', 'col')), may hold values from -1 to 191, as said below
Outputs:
- square_tiles: bfloat16 [192, 8, 2, 128, 128], P(('row', 'col'), None, None, 'layer')
Inputs may be any that keep to these rules, and one draw needn't show every extreme that they name: `tile_columns`: entry [i, g, s] is a tile column in group g (columns g * 24 to (g + 1) * 24 - 1) or -1; within one block row and group the listed columns are distinct and empty slots come after the listed ones; block row i lists its own column i in the first slot of its group, whose 2 slots are all listed; other groups hold 0 to 2 listed tiles.
All inputs are finite; a program needn't handle non-finite values.
Results may differ from a plain program's by a relative error of at most 0.0048.
Values may be sent and summed in bfloat16 or wider, within the bound.
No kernel may reach another device: no remote copies, remote signals or barrier semaphores. Data moves between devices by JAX's collectives and lax.ppermute only.
A program may use at most 64 MiB of HBM per device.

v0:
```python
import jax
import jax.numpy as jnp
from jax import lax
from jax.sharding import Mesh
from jax.sharding import PartitionSpec as P

ROW = ("row_0", "row_1")
ROW_COL = ("row_0", "row_1", "col")


def filled_up(lines, devices):
    spare = -len(lines) % devices
    return jnp.pad(lines, [(0, spare)] + [(0, 0)] * (lines.ndim - 1))


def spread(array, axis, root):
    lines = jnp.where(lax.axis_index(axis) == root, array, jnp.zeros_like(array)).reshape(
        -1, *array.shape[1:][-1:]
    )
    padded = filled_up(lines, lax.axis_size(axis))
    own = lax.psum_scatter(padded, axis, scatter_dimension=0, tiled=True)
    return lax.all_gather(own, axis, axis=0, tiled=True)[: len(lines)].reshape(array.shape)


def broadcast_by_axis(array, axes, root):
    array = jnp.where(lax.axis_index(axes) == root, array, jnp.zeros_like(array))
    for axis in axes:
        array = lax.psum(array, axis)
    return array


def in_blocks(array, dim, devices):
    before, after = (array.shape[:dim], array.shape[dim + 1 :])
    return jnp.moveaxis(array.reshape(*before, devices, -1, *after), dim, 0)


def sent_and_summed(array, axis, dim):
    pieces = in_blocks(array, dim, lax.axis_size(axis))
    arrived = lax.all_to_all(pieces, axis, split_axis=0, concat_axis=0, tiled=True)
    return arrived.astype(jnp.float32).sum(axis=0)


def multiply(left_tiles, left_columns, right_tiles, right_columns, target_columns, start_row):
    is_live = left_columns >= 0
    inner_rows = jnp.where(is_live, left_columns - start_row, 0).astype(jnp.int32)
    inner_columns = right_columns[inner_rows]
    matches = (
        (inner_columns[:, :, None, :] == target_columns[:, None, :, None])
        & is_live[:, :, None, None]
        & (target_columns >= 0)[:, None, :, None]
    )
    slot_index = jnp.argmax(matches.astype(jnp.int32), axis=-1)
    located = jnp.any(matches, axis=-1)
    selected = right_tiles[inner_rows[:, :, None], slot_index]
    selected = jnp.where(located[:, :, :, None, None], selected, jnp.zeros((), jnp.bfloat16))
    return jnp.einsum("iarc,iascd->isrd", left_tiles, selected, preferred_element_type=jnp.float32)


def on_device(density_tiles, tile_columns):
    row_count = lax.axis_size(ROW)
    column_count = lax.axis_size("col")
    layer_count = lax.axis_size("layer")
    grid_tiles, grid_columns = (
        lax.all_to_all(density_tiles, "col", split_axis=1, concat_axis=0, tiled=True),
        lax.all_to_all(tile_columns, "col", split_axis=1, concat_axis=0, tiled=True),
    )
    block_tiles = grid_tiles[:, 0]
    block_columns = grid_columns[:, 0]
    group_rows = block_tiles.shape[0]
    row_ratio = column_count // row_count
    panel_rows = group_rows // row_ratio
    per_layer = column_count // layer_count
    layer_index = lax.axis_index("layer")
    partial_value = jnp.zeros(block_tiles.shape, jnp.float32)
    for panel_step in range(per_layer):
        panel_index = layer_index * per_layer + panel_step
        left_tiles, left_columns = (
            spread(block_tiles, "col", panel_index),
            spread(block_columns, "col", panel_index),
        )
        right_tiles, right_columns = (
            broadcast_by_axis(block_tiles, ROW, panel_index // row_ratio),
            broadcast_by_axis(block_columns, ROW, panel_index // row_ratio),
        )
        partial_value = partial_value + multiply(
            left_tiles,
            left_columns,
            right_tiles,
            right_columns,
            block_columns,
            panel_index * panel_rows,
        )
    rounded = partial_value.astype(jnp.bfloat16)
    summed = sent_and_summed(rounded.astype(jnp.float32).astype(jnp.bfloat16), "layer", 2)
    returned = lax.all_to_all(
        summed.astype(jnp.bfloat16)[:, None], "col", split_axis=0, concat_axis=1, tiled=True
    )
    return returned


def solution(mesh):
    split = Mesh(
        mesh.devices.reshape(4, 2, mesh.shape["col"], mesh.shape["layer"]),
        ("row_0", "row_1", "col", "layer"),
    )
    return jax.shard_map(
        on_device,
        mesh=split,
        in_specs=(P(ROW_COL, None, None, None, None), P(ROW_COL, None, None)),
        out_specs=P(ROW_COL, None, None, "layer", None),
        check_vma=False,
    )
```

profile of v0, /device:TPU:1, one launch (start us, length us, event | category | flops | bytes accessed | tf_op | source)
XLA Modules:
  0.0 319.0 jit_solution(11141987187466286460)
XLA Ops:
  7.4 2.7 copy.204
  10.1 10.0 %all-to-all-start.1 = ((bf16[3,8,2,128,128]{4,3,2,0,1:T(8,128)(2,1)}), bf16[3,8,2,128,128]{4,3,2,0,1:T(8,128)(2,1)S(1)}, u32[]{:S(2)}, u32[]{:S(2)}) async-start(bf16[3,8,2,128,128]{4,3,2,0,1:T(8,128)(2,1)} %copy.204), calls=%async_computation.1 | async-start | bytes 3145728 | tf_op jit(solution)/shard_map/all_to_all | solution.py:64
  20.1 33.3 %all-to-all-done.1 = bf16[3,8,2,128,128]{4,3,2,0,1:T(8,128)(2,1)S(1)} async-done(((bf16[3,8,2,128,128]{4,3,2,0,1:T(8,128)(2,1)}), bf16[3,8,2,128,128]{4,3,2,0,1:T(8,128)(2,1)S(1)}, u32[]{:S(2)}, u32[]{:S(2)}) %all-to-all-start.1) | async-done | bytes 1572896 | tf_op jit(solution)/shard_map/all_to_all | solution.py:64
  53.4 2.8 broadcast_select_fusion.2
  56.3 0.5 reduce-scatter.5.cloned.1.call-update
  56.8 0.5 reduce-scatter.3.cloned.1.call-update
  57.4 82.9 %all-reduce.10.cloned.1.call-done = (bf16[24,2,128,128]{3,2,1,0:T(8,128)(2,1)}, bf16[24,2,128,128]{3,2,1,0:T(8,128)(2,1)}) async-done(((bf16[24,2,128,128]{3,2,1,0:T(8,128)(2,1)}, bf16[24,2,128,128]{3,2,1,0:T(8,128)(2,1)}), (bf16[24,2,128,128]{3,2,1,0:T(8,128)(2,1)}, bf16[24,2,128,128]{3,2,1,0:T(8,128)(2,1)})) %all-reduce.10.cloned.1.call-update) | async-done | bytes 3145744 | tf_op jit(solution)/shard_map/psum | solution.py:28
  140.4 0.5 all-gather.7.cloned.1.call-update
  140.9 0.1 copy-done
  141.0 0.7 copy.187
  141.7 7.8 %all-to-all-start = ((s32[3,8,2]{0,2,1:T(2,128)}), s32[3,8,2]{0,2,1:T(2,128)S(1)}, u32[]{:S(2)}, u32[]{:S(2)}) async-start(s32[3,8,2]{0,2,1:T(2,128)} %copy.187), calls=%async_computation | async-start | bytes 16384 | tf_op jit(solution)/shard_map/all_to_all | solution.py:65
  149.5 0.6 dynamic-slice
  150.7 5.9 %all-to-all-done = s32[3,8,2]{0,2,1:T(2,128)S(1)} async-done(((s32[3,8,2]{0,2,1:T(2,128)}), s32[3,8,2]{0,2,1:T(2,128)S(1)}, u32[]{:S(2)}, u32[]{:S(2)}) %all-to-all-start) | async-done | bytes 224 | tf_op jit(solution)/shard_map/all_to_all | solution.py:65
  156.6 0.1 squeeze.4
  156.7 0.1 copy.190
  156.8 25.1 %all-reduce.2 = (s32[24,2]{1,0:T(8,128)S(1)}, s32[24,2]{1,0:T(8,128)S(1)}) all-reduce(s32[24,2]{1,0:T(8,128)S(1)} %get-tuple-element.32, s32[24,2]{1,0:T(8,128)S(1)} %get-tuple-element.34), channel_id=4, replica_groups=mesh['row_0'=4,'row_1'=2,'col'=8,'layer'=4] {'col'}, use_global_device_ids=true, to_apply=%region_10.11.clone | all-reduce | flops 96 | bytes 768
  181.9 0.1 copy.192
  182.0 12.9 %all-gather = s32[8,3,2]{1,2,0:T(2,128)S(1)} all-gather(s32[1,3,2]{1,2,0:T(2,128)S(1)} %bitcast.110), channel_id=1, replica_groups=mesh['row_0'=4,'row_1'=2,'col'=8,'layer'=4] {'col'}, dimensions={0}, use_global_device_ids=true | all-gather | bytes 216 | tf_op jit(solution)/shard_map/all_gather | solution.py:22
  194.9 0.1 copy.193
  195.1 0.1 copy.202
  195.2 0.1 copy.210
  195.3 0.1 copy.194
  195.4 0.1 reshape.112
  195.5 0.1 copy.197
  195.6 0.1 copy.196
  195.6 0.1 reshape.114
  195.7 13.0 %all-gather.1 = s32[8,3,2]{1,2,0:T(2,128)S(1)} all-gather(s32[1,3,2]{1,2,0:T(2,128)S(1)} %bitcast.109), channel_id=1, replica_groups=mesh['row_0'=4,'row_1'=2,'col'=8,'layer'=4] {'col'}, dimensions={0}, use_global_device_ids=true | all-gather | bytes 216 | tf_op jit(solution)/shard_map/all_gather | solution.py:22
  208.7 0.1 copy.211
  208.8 0.1 copy.212
  208.9 0.1 reshape.116
  209.0 0.1 copy.215
  209.1 0.1 copy.214
  209.2 0.1 reshape.118
  209.3 0.1 copy.216
  209.4 0.1 copy.220
  209.5 0.1 reshape.81
  209.6 13.5 %all-reduce.3 = (s32[24,2]{1,0:T(8,128)S(1)}, s32[24,2]{1,0:T(8,128)S(1)}) all-reduce(s32[24,2]{1,0:T(8,128)S(1)} %get-tuple-element.33, s32[24,2]{1,0:T(8,128)S(1)} %get-tuple-element.31), channel_id=1, replica_groups=mesh['row_0'=4,'row_1'=2,'col'=8,'layer'=4] {'row_0'}, use_global_device_ids=true, to_apply=%region_8.9 | all-reduce | flops 96 | bytes 768 | tf_op jit(solution)/shard_map/psum | solution.py:28
  223.0 7.7 %all-reduce.4 = (s32[24,2]{1,0:T(8,128)S(1)}, s32[24,2]{1,0:T(8,128)S(1)}) all-reduce(s32[24,2]{1,0:T(8,128)S(1)} %get-tuple-element.11, s32[24,2]{1,0:T(8,128)S(1)} %get-tuple-element.12), channel_id=1, replica_groups=mesh['row_0'=4,'row_1'=2,'col'=8,'layer'=4] {'row_1'}, use_global_device_ids=true, to_apply=%region_9.10 | all-reduce | flops 96 | bytes 768 | tf_op jit(solution)/shard_map/psum | solution.py:28
  230.7 0.6 gather_fusion.2
  231.3 0.1 copy.218
  231.4 0.1 copy.198
  231.5 0.1 copy.205
  231.6 0.1 reshape.67
  231.7 0.6 gather_fusion
  232.3 0.1 copy.200
  232.4 0.1 copy.203
  232.5 0.1 copy.219
  232.7 0.6 iota_reduce_fusion
  233.3 0.1 copy.221
  233.4 0.1 reshape.87
  233.5 0.6 iota_reduce_fusion.1
  234.2 0.1 copy.206
  234.3 0.1 reshape.73
  234.4 11.8 %all-reduce.12.cloned.1.call-done = (bf16[24,2,128,128]{3,2,1,0:T(8,128)(2,1)}, bf16[24,2,128,128]{3,2,1,0:T(8,128)(2,1)}) async-done(((bf16[24,2,128,128]{3,2,1,0:T(8,128)(2,1)}, bf16[24,2,128,128]{3,2,1,0:T(8,128)(2,1)}), (bf16[24,2,128,128]{3,2,1,0:T(8,128)(2,1)}, bf16[24,2,128,128]{3,2,1,0:T(8,128)(2,1)})) %all-reduce.12.cloned.1.call-update) | async-done | bytes 3145744 | tf_op jit(solution)/shard_map/psum | solution.py:28
  246.2 4.5 %gather_fusion.3 = bf16[96,128,128]{2,1,0:T(8,128)(2,1)} fusion(bf16[24,2,128,128]{3,2,1,0:T(8,128)(2,1)} %get-tuple-element.17, s32[96]{0:T(128)S(1)} %reshape.87), kind=kCustom, calls=%fused_computation.3 | custom fusion | bytes 6292224 | tf_op jit(solution)/shard_map/gather | solution.py:54
  250.6 3.0 gather_fusion.1
  253.7 4.8 %fusion.1 = f32[24,2,128,128,1]{2,3,1,4,0:T(8,128)} fusion(bf16[24,2,128,128,1]{3,2,4,1,0:T(8,128)(2,1)} %bitcast.105, bf16[24,2,2,128,128]{4,3,2,1,0:T(8,128)(2,1)} %bitcast.95, pred[24,2,2]{2,1,0:T(4,128)(4,1)S(1)} %copy.219), kind=kOutput, calls=%fused_computation.6 | convolution fusion | flops 404226048 | bytes 7864416 | tf_op jit(solution)/shard_map/iarc,iascd->isrd/dot_general | solution.py:56
  258.5 5.5 %all-gather.5.cloned.1.call-done = bf16[6144,128]{1,0:T(8,128)(2,1)} async-done(((bf16[768,128]{1,0:T(8,128)(2,1)}), bf16[6144,128]{1,0:T(8,128)(2,1)}) %all-gather.5.cloned.1.call-update) | async-done | bytes 1572880 | tf_op jit(solution)/shard_map/all_gather | solution.py:22
  263.9 3.0 fusion
  267.0 0.4 copy.235
  267.4 24.0 %all_to_all.47 = bf16[4,24,2,32,128]{4,3,2,1,0:T(8,128)(2,1)S(1)} all-to-all(bf16[4,24,2,32,128]{4,3,2,1,0:T(8,128)(2,1)S(1)} %bitcast.97), channel_id=1, replica_groups=mesh['row_0'=4,'row_1'=2,'col'=8,'layer'=4] {'layer'}, dimensions={0} | all-to-all | bytes 3145728 | tf_op jit(solution)/shard_map/all_to_all | solution.py:39
  291.4 0.3 reduce_sum.12
  291.8 18.9 %all_to_all.48 = bf16[24,1,2,32,128]{4,3,2,1,0:T(8,128)(2,1)S(1)} all-to-all(bf16[24,1,2,32,128]{4,3,2,1,0:T(8,128)(2,1)S(1)} %bitcast.104), channel_id=1, replica_groups=mesh['row_0'=4,'row_1'=2,'col'=8,'layer'=4] {'col'}, dimensions={0} | all-to-all | bytes 786432 | tf_op jit(solution)/shard_map/all_to_all | solution.py:95
  310.6 0.8 copy.224
  (30 shorter events, 0.4 us)
Async XLA Ops:
  10.1 43.3 %all-to-all-start.1 = ((bf16[3,8,2,128,128]{4,3,2,0,1:T(8,128)(2,1)}), bf16[3,8,2,128,128]{4,3,2,0,1:T(8,128)(2,1)S(1)}, u32[]{:S(2)}, u32[]{:S(2)}) async-start(bf16[3,8,2,128,128]{4,3,2,0,1:T(8,128)(2,1)} %copy.204), calls=%async_computation.1 | async-start | bytes 3145728 | tf_op jit(solution)/shard_map/all_to_all | solution.py:64
  20.1 120.3 %all-reduce.10.cloned.1.call-start = ((), (), s32[]{:S(2)}) async-start(), calls=%async_computation.10 | async-start | bytes 6291456 | tf_op jit(solution)/shard_map/psum | solution.py:28
  56.2 84.2 %reduce-scatter.5.cloned.1.call-start = ((), (), s32[]{:S(2)}) async-start(), calls=%async_computation.8 | async-start | bytes 1769472 | tf_op jit(solution)/shard_map/reduce_scatter | solution.py:21
  56.8 138.2 %reduce-scatter.3.cloned.1.call-start = ((), (), s32[]{:S(2)}) async-start(), calls=%async_computation.6 | async-start | bytes 1769472 | tf_op jit(solution)/shard_map/reduce_scatter | solution.py:21
  57.4 188.8 %all-reduce.12.cloned.1.call-start = ((), (), s32[]{:S(2)}) async-start(), calls=%async_computation.11 | async-start | bytes 6291456 | tf_op jit(solution)/shard_map/psum | solution.py:28
  140.3 0.7 copy-start
  140.3 9.2 %copy-start.1 = (u32[256]{0:T(256)S(1)}, u32[256]{0:T(256)}, u32[]{:S(2)}) copy-start(u32[256]{0:T(256)} %constant.100) | copy-start | bytes 3076
  140.3 113.3 %all-gather.7.cloned.1.call-start = ((), (), s32[]{:S(2)}) async-start(), calls=%async_computation.9 | async-start | bytes 1769472 | tf_op jit(solution)/shard_map/all_gather | solution.py:22
  141.7 14.9 %all-to-all-start = ((s32[3,8,2]{0,2,1:T(2,128)}), s32[3,8,2]{0,2,1:T(2,128)S(1)}, u32[]{:S(2)}, u32[]{:S(2)}) async-start(s32[3,8,2]{0,2,1:T(2,128)} %copy.187), calls=%async_computation | async-start | bytes 16384 | tf_op jit(solution)/shard_map/all_to_all | solution.py:65
  149.5 114.4 %all-gather.5.cloned.1.call-start = ((), (), s32[]{:S(2)}) async-start(), calls=%async_computation.7 | async-start | bytes 1769472 | tf_op jit(solution)/shard_map/all_gather | solution.py:22
Sparse Core Ops, SparseCore 0:
  56.3 83.9 all-reduce.9
  143.0 103.1 all-reduce.11
Sparse Core Ops, SparseCore 1:
  59.3 43.9 reduce-scatter.4
  105.7 40.1 reduce-scatter.2
  147.6 63.6 all-gather.6
  213.1 50.8 all-gather.4
where the time goes:
time: 319 us
  waiting for transfers between devices  141 us (44%)
  blocking collectives  115 us (36%)
  starting transfers between devices  18 us (6%)
  local copies, waits for them, and re-layouts  16.9 us (5%)
  between operations  15.8 us (5%)
  matrix products  7.82 us (2%)
  other arithmetic  4.51 us (1%)
    psum x2, waiting for transfers between devices, broadcast_by_axis(): array = lax.psum(array, axis)  94.7 us
    all_to_all x1, waiting for transfers between devices, on_device(): lax.all_to_all(density_tiles, 'col', split_axis=1, concat_axis=0, tiled=T...  33.3 us
    all_gather x2, blocking collectives, spread(): lax.all_gather(own, axis, axis=0, tiled=True)[:len(lines)]  25.9 us
    unnamed x1, blocking collectives  25.1 us
    all_to_all x1, blocking collectives, sent_and_summed(): lax.all_to_all(pieces, axis, split_axis=0, concat_axis=0, tiled=True)  24 us
    psum x2, blocking collectives, broadcast_by_axis(): array = lax.psum(array, axis)  21.2 us
    all_to_all x1, blocking collectives, on_device(): lax.all_to_all(summed.astype(jnp.bfloat16)[:, None], 'col', split_axis=0,...  18.9 us
    all_to_all x1, starting transfers between devices, on_device(): lax.all_to_all(density_tiles, 'col', split_axis=1, concat_axis=0, tiled=T...  9.95 us
  transfers between devices with their start and end apart: 8, of which 5 were waited for; matrix products, arithmetic and copies ran while one was open for 6% of the time, Pallas kernels for 0%

commit v1 on v0

--- a/solution.py
+++ b/solution.py
@@ -61,7 +61,12 @@
     column_count = lax.axis_size("col")
     layer_count = lax.axis_size("layer")
     grid_tiles, grid_columns = (
-        lax.all_to_all(density_tiles, "col", split_axis=1, concat_axis=0, tiled=True),
+        jnp.concatenate(
+            lax.all_to_all(
+                jnp.stack(jnp.split(density_tiles, lax.axis_size("col"), axis=1)), "col", 0, 0
+            ),
+            axis=0,
+        ),
         lax.all_to_all(tile_columns, "col", split_axis=1, concat_axis=0, tiled=True),
     )
     block_tiles = grid_tiles[:, 0]

time: 319 us -> 330 us (1.034)
  local copies, waits for them, and re-layouts: 16.9 us -> 27.1 us
    unnamed x8 -> x14, local copies, waits for them, and re-layouts: 4.1 us -> 12.6 us
where the time goes in v1:
time: 330 us; the launch traced here: 329 us
  waiting for transfers between devices  141 us (43%)
  blocking collectives  115 us (35%)
  local copies, waits for them, and re-layouts  27.1 us (8%)
  starting transfers between devices  18 us (5%)
  between operations  15.8 us (5%)
  matrix products  7.82 us (2%)
  other arithmetic  4.51 us (1%)
    psum x2, waiting for transfers between devices, broadcast_by_axis(): array = lax.psum(array, axis)  94.7 us
    all_to_all x1, waiting for transfers between devices, on_device(): lax.all_to_all(jnp.stack(jnp.split(density_tiles, lax.axis_size('col'), a...  33.3 us
    all_gather x2, blocking collectives, spread(): lax.all_gather(own, axis, axis=0, tiled=True)[:len(lines)]  25.9 us
    unnamed x1, blocking collectives  25.1 us
    all_to_all x1, blocking collectives, sent_and_summed(): lax.all_to_all(pieces, axis, split_axis=0, concat_axis=0, tiled=True)  24 us
    psum x2, blocking collectives, broadcast_by_axis(): array = lax.psum(array, axis)  21.2 us
    all_to_all x1, blocking collectives, on_device(): lax.all_to_all(summed.astype(jnp.bfloat16)[:, None], 'col', split_axis=0,...  18.9 us
    unnamed x14, local copies, waits for them, and re-layouts  12.6 us
  transfers between devices with their start and end apart: 8, of which 5 were waited for; matrix products, arithmetic and copies ran while one was open for 6% of the time, Pallas kernels for 0%

profile of v1, /device:TPU:1, one launch (start us, length us, event | category | flops | bytes accessed | tf_op | source)
XLA Modules:
  0.0 329.2 jit_solution(4951035234215629630)
XLA Ops:
  7.4 1.6 bitcast_dynamic-update-slice_fusion.6
  9.0 1.6 bitcast_dynamic-update-slice_fusion.5
  10.6 1.6 bitcast_dynamic-update-slice_fusion.4
  12.2 1.6 bitcast_dynamic-update-slice_fusion.3
  13.8 1.6 bitcast_dynamic-update-slice_fusion.2
  15.4 1.6 bitcast_dynamic-update-slice_fusion.7
  17.0 1.6 bitcast_dynamic-update-slice_fusion.1
  18.7 1.6 bitcast_dynamic-update-slice_fusion
  20.3 10.0 %all-to-all-start.1 = ((bf16[8,3,1,2,128,128]{5,4,3,1,2,0:T(8,128)(2,1)}), bf16[8,3,1,2,128,128]{5,4,3,1,2,0:T(8,128)(2,1)S(1)}, u32[]{:S(2)}, u32[]{:S(2)}) async-start(bf16[8,3,1,2,128,128]{5,4,3,1,2,0:T(8,128)(2,1)} %bitcast_dynamic-update-slice_fusion), calls=%async_computation.1 | async-start | bytes 3145728 | tf_op jit(solution)/shard_map/all_to_all | solution.py:65
  30.2 33.3 %all-to-all-done.1 = bf16[8,3,1,2,128,128]{5,4,3,1,2,0:T(8,128)(2,1)S(1)} async-done(((bf16[8,3,1,2,128,128]{5,4,3,1,2,0:T(8,128)(2,1)}), bf16[8,3,1,2,128,128]{5,4,3,1,2,0:T(8,128)(2,1)S(1)}, u32[]{:S(2)}, u32[]{:S(2)}) %all-to-all-start.1) | async-done | bytes 1572896 | tf_op jit(solution)/shard_map/all_to_all | solution.py:65
  63.6 2.8 broadcast_select_fusion.2
  66.5 0.5 reduce-scatter.5.cloned.1.call-update
  67.0 0.5 reduce-scatter.3.cloned.1.call-update
  67.6 82.9 %all-reduce.10.cloned.1.call-done = (bf16[24,2,128,128]{3,2,1,0:T(8,128)(2,1)}, bf16[24,2,128,128]{3,2,1,0:T(8,128)(2,1)}) async-done(((bf16[24,2,128,128]{3,2,1,0:T(8,128)(2,1)}, bf16[24,2,128,128]{3,2,1,0:T(8,128)(2,1)}), (bf16[24,2,128,128]{3,2,1,0:T(8,128)(2,1)}, bf16[24,2,128,128]{3,2,1,0:T(8,128)(2,1)})) %all-reduce.10.cloned.1.call-update) | async-done | bytes 3145744 | tf_op jit(solution)/shard_map/psum | solution.py:28
  150.6 0.5 all-gather.7.cloned.1.call-update
  151.2 0.7 copy.218
  151.9 7.8 %all-to-all-start = ((s32[3,8,2]{0,2,1:T(2,128)}), s32[3,8,2]{0,2,1:T(2,128)S(1)}, u32[]{:S(2)}, u32[]{:S(2)}) async-start(s32[3,8,2]{0,2,1:T(2,128)} %copy.218), calls=%async_computation | async-start | bytes 16384 | tf_op jit(solution)/shard_map/all_to_all | solution.py:70
  159.7 0.6 dynamic-slice
  160.9 5.9 %all-to-all-done = s32[3,8,2]{0,2,1:T(2,128)S(1)} async-done(((s32[3,8,2]{0,2,1:T(2,128)}), s32[3,8,2]{0,2,1:T(2,128)S(1)}, u32[]{:S(2)}, u32[]{:S(2)}) %all-to-all-start) | async-done | bytes 224 | tf_op jit(solution)/shard_map/all_to_all | solution.py:70
  166.8 0.1 copy.221
  166.9 25.1 %all-reduce.2 = (s32[24,2]{1,0:T(8,128)S(1)}, s32[24,2]{1,0:T(8,128)S(1)}) all-reduce(s32[24,2]{1,0:T(8,128)S(1)} %get-tuple-element.32, s32[24,2]{1,0:T(8,128)S(1)} %get-tuple-element.34), channel_id=4, replica_groups=mesh['row_0'=4,'row_1'=2,'col'=8,'layer'=4] {'col'}, use_global_device_ids=true, to_apply=%region_10.11.clone | all-reduce | flops 96 | bytes 768
  192.1 0.1 copy.223
  192.2 12.9 %all-gather = s32[8,3,2]{1,2,0:T(2,128)S(1)} all-gather(s32[1,3,2]{1,2,0:T(2,128)S(1)} %bitcast.124), channel_id=1, replica_groups=mesh['row_0'=4,'row_1'=2,'col'=8,'layer'=4] {'col'}, dimensions={0}, use_global_device_ids=true | all-gather | bytes 216 | tf_op jit(solution)/shard_map/all_gather | solution.py:22
  205.1 0.1 copy.224
  205.3 0.1 copy.233
  205.3 0.1 copy.247
  205.4 0.1 copy.225
  205.5 0.1 reshape.99
  205.6 0.1 copy.228
  205.7 0.1 copy.227
  205.9 13.0 %all-gather.1 = s32[8,3,2]{1,2,0:T(2,128)S(1)} all-gather(s32[1,3,2]{1,2,0:T(2,128)S(1)} %bitcast.123), channel_id=1, replica_groups=mesh['row_0'=4,'row_1'=2,'col'=8,'layer'=4] {'col'}, dimensions={0}, use_global_device_ids=true | all-gather | bytes 216 | tf_op jit(solution)/shard_map/all_gather | solution.py:22
  218.9 0.1 copy.248
  219.0 0.1 copy.249
  219.1 0.1 reshape.103
  219.2 0.1 copy.252
  219.3 0.1 copy.251
  219.5 0.1 copy.253
  219.6 0.1 reshape.68
  219.7 13.5 %all-reduce.3 = (s32[24,2]{1,0:T(8,128)S(1)}, s32[24,2]{1,0:T(8,128)S(1)}) all-reduce(s32[24,2]{1,0:T(8,128)S(1)} %get-tuple-element.33, s32[24,2]{1,0:T(8,128)S(1)} %get-tuple-element.31), channel_id=1, replica_groups=mesh['row_0'=4,'row_1'=2,'col'=8,'layer'=4] {'row_0'}, use_global_device_ids=true, to_apply=%region_8.9 | all-reduce | flops 96 | bytes 768 | tf_op jit(solution)/shard_map/psum | solution.py:28
  233.2 7.7 %all-reduce.4 = (s32[24,2]{1,0:T(8,128)S(1)}, s32[24,2]{1,0:T(8,128)S(1)}) all-reduce(s32[24,2]{1,0:T(8,128)S(1)} %get-tuple-element.11, s32[24,2]{1,0:T(8,128)S(1)} %get-tuple-element.12), channel_id=1, replica_groups=mesh['row_0'=4,'row_1'=2,'col'=8,'layer'=4] {'row_1'}, use_global_device_ids=true, to_apply=%region_9.10 | all-reduce | flops 96 | bytes 768 | tf_op jit(solution)/shard_map/psum | solution.py:28
  240.9 0.6 gather_fusion.2
  241.5 0.1 copy.255
  241.8 0.1 reshape.54
  241.9 0.6 gather_fusion
  242.5 0.1 copy.231
  242.6 0.1 copy.234
  242.7 0.1 copy.256
  242.8 0.6 iota_reduce_fusion
  243.5 0.1 copy.258
  243.6 0.1 reshape.74
  243.7 0.6 iota_reduce_fusion.1
  244.4 0.1 copy.243
  244.5 0.1 reshape.60
  244.6 11.8 %all-reduce.12.cloned.1.call-done = (bf16[24,2,128,128]{3,2,1,0:T(8,128)(2,1)}, bf16[24,2,128,128]{3,2,1,0:T(8,128)(2,1)}) async-done(((bf16[24,2,128,128]{3,2,1,0:T(8,128)(2,1)}, bf16[24,2,128,128]{3,2,1,0:T(8,128)(2,1)}), (bf16[24,2,128,128]{3,2,1,0:T(8,128)(2,1)}, bf16[24,2,128,128]{3,2,1,0:T(8,128)(2,1)})) %all-reduce.12.cloned.1.call-update) | async-done | bytes 3145744 | tf_op jit(solution)/shard_map/psum | solution.py:28
  256.4 4.5 %gather_fusion.3 = bf16[96,128,128]{2,1,0:T(8,128)(2,1)} fusion(bf16[24,2,128,128]{3,2,1,0:T(8,128)(2,1)} %get-tuple-element.17, s32[96]{0:T(128)S(1)} %reshape.74), kind=kCustom, calls=%fused_computation.3 | custom fusion | bytes 6292224 | tf_op jit(solution)/shard_map/gather | solution.py:54
  260.8 3.0 gather_fusion.1
  263.8 4.8 %fusion.1 = f32[24,2,128,128,1]{2,3,1,4,0:T(8,128)} fusion(bf16[24,2,128,128,1]{3,2,4,1,0:T(8,128)(2,1)} %bitcast.119, bf16[24,2,2,128,128]{4,3,2,1,0:T(8,128)(2,1)} %bitcast.109, pred[24,2,2]{2,1,0:T(4,128)(4,1)S(1)} %copy.256), kind=kOutput, calls=%fused_computation.6 | convolution fusion | flops 404226048 | bytes 7864416 | tf_op jit(solution)/shard_map/iarc,iascd->isrd/dot_general | solution.py:56
  268.6 5.5 %all-gather.5.cloned.1.call-done = bf16[6144,128]{1,0:T(8,128)(2,1)} async-done(((bf16[768,128]{1,0:T(8,128)(2,1)}), bf16[6144,128]{1,0:T(8,128)(2,1)}) %all-gather.5.cloned.1.call-update) | async-done | bytes 1572880 | tf_op jit(solution)/shard_map/all_gather | solution.py:22
  274.1 3.0 fusion
  277.2 0.4 copy.279
  277.6 24.0 %all_to_all.43 = bf16[4,24,2,32,128]{4,3,2,1,0:T(8,128)(2,1)S(1)} all-to-all(bf16[4,24,2,32,128]{4,3,2,1,0:T(8,128)(2,1)S(1)} %bitcast.111), channel_id=1, replica_groups=mesh['row_0'=4,'row_1'=2,'col'=8,'layer'=4] {'layer'}, dimensions={0} | all-to-all | bytes 3145728 | tf_op jit(solution)/shard_map/all_to_all | solution.py:39
  301.6 0.3 reduce_sum.12
  301.9 18.9 %all_to_all.44 = bf16[24,1,2,32,128]{4,3,2,1,0:T(8,128)(2,1)S(1)} all-to-all(bf16[24,1,2,32,128]{4,3,2,1,0:T(8,128)(2,1)S(1)} %bitcast.118), channel_id=1, replica_groups=mesh['row_0'=4,'row_1'=2,'col'=8,'layer'=4] {'col'}, dimensions={0} | all-to-all | bytes 786432 | tf_op jit(solution)/shard_map/all_to_all | solution.py:100
  320.8 0.8 copy.261
  (37 shorter events, 1.0 us)
Async XLA Ops:
  20.3 43.3 %all-to-all-start.1 = ((bf16[8,3,1,2,128,128]{5,4,3,1,2,0:T(8,128)(2,1)}), bf16[8,3,1,2,128,128]{5,4,3,1,2,0:T(8,128)(2,1)S(1)}, u32[]{:S(2)}, u32[]{:S(2)}) async-start(bf16[8,3,1,2,128,128]{5,4,3,1,2,0:T(8,128)(2,1)} %bitcast_dynamic-update-slice_fusion), calls=%async_computation.1 | async-start | bytes 3145728 | tf_op jit(solution)/shard_map/all_to_all | solution.py:65
  30.2 120.3 %all-reduce.10.cloned.1.call-start = ((), (), s32[]{:S(2)}) async-start(), calls=%async_computation.10 | async-start | bytes 6291456 | tf_op jit(solution)/shard_map/psum | solution.py:28
  66.4 84.2 %reduce-scatter.5.cloned.1.call-start = ((), (), s32[]{:S(2)}) async-start(), calls=%async_computation.8 | async-start | bytes 1769472 | tf_op jit(solution)/shard_map/reduce_scatter | solution.py:21
  67.0 138.2 %reduce-scatter.3.cloned.1.call-start = ((), (), s32[]{:S(2)}) async-start(), calls=%async_computation.6 | async-start | bytes 1769472 | tf_op jit(solution)/shard_map/reduce_scatter | solution.py:21
  67.6 188.8 %all-reduce.12.cloned.1.call-start = ((), (), s32[]{:S(2)}) async-start(), calls=%async_computation.11 | async-start | bytes 6291456 | tf_op jit(solution)/shard_map/psum | solution.py:28
  150.5 0.7 copy-start
  150.5 9.2 %copy-start.1 = (u32[256]{0:T(256)S(1)}, u32[256]{0:T(256)}, u32[]{:S(2)}) copy-start(u32[256]{0:T(256)} %constant.100) | copy-start | bytes 3076
  150.5 113.3 %all-gather.7.cloned.1.call-start = ((), (), s32[]{:S(2)}) async-start(), calls=%async_computation.9 | async-start | bytes 1769472 | tf_op jit(solution)/shard_map/all_gather | solution.py:22
  151.9 14.9 %all-to-all-start = ((s32[3,8,2]{0,2,1:T(2,128)}), s32[3,8,2]{0,2,1:T(2,128)S(1)}, u32[]{:S(2)}, u32[]{:S(2)}) async-start(s32[3,8,2]{0,2,1:T(2,128)} %copy.218), calls=%async_computation | async-start | bytes 16384 | tf_op jit(solution)/shard_map/all_to_all | solution.py:70
  159.7 114.4 %all-gather.5.cloned.1.call-start = ((), (), s32[]{:S(2)}) async-start(), calls=%async_computation.7 | async-start | bytes 1769472 | tf_op jit(solution)/shard_map/all_gather | solution.py:22
Sparse Core Ops, SparseCore 0:
  66.5 83.9 all-reduce.9
  153.1 103.1 all-reduce.11
Sparse Core Ops, SparseCore 1:
  69.4 43.9 reduce-scatter.4
  115.9 40.1 reduce-scatter.2
  157.7 63.6 all-gather.6
  223.3 50.8 all-gather.4
